TPU v7x, 32 devices: a whole 2x2x4 slice. The times are simulated.
32 devices in a mesh: rep: 4 (over x, y), dp: 8 (over z, core).
Axes of the slice: x: 2, y: 2, z: 4, core: 2. Of those that a mesh axis runs over, the one named last changes fastest.
Arguments:
- a: bfloat16 [32, 4, 8192, 1280], P(('rep', 'dp')), parts along dimension 0
- g: bfloat16 [32, 4, 8192, 3072], P(('rep', 'dp')), parts along dimension 0
Outputs:
- output: bfloat16 [16, 1280, 3072], P('rep'), parts along dimension 0
There are 4 independent parts. A program takes and returns all parts, laid end to end along the dimension named above; each array names one.
All inputs are finite; a program needn't handle non-finite values.
Results may differ from a plain program's by a relative error of at most 0.012.
Values are sent between devices in bfloat16 or wider.
A program may use at most 2 GiB of HBM per device.

v0:
```python
import jax
import jax.numpy as jnp


def solution(mesh):
    groups = mesh.shape["rep"]

    def step(a, g):
        a, g = (t.reshape(groups, -1, *t.shape[1:]) for t in (a, g))
        sums = jnp.einsum("rsntd,rsntf->rndf", a, g, preferred_element_type=jnp.float32)
        return sums.astype(jnp.bfloat16).reshape(-1, *sums.shape[2:])

    return step
```

profile of v0, /device:TPU:3, one launch (start us, length us, event | category | flops | bytes accessed | tf_op | source)
XLA Modules:
  0.0 1482.3 jit_solution(6604110702986602316)
XLA Ops:
  0.0 276.7 %fusion.3 = f32[1,4,1280,3072]{3,2,1,0:T(8,128)} fusion(bf16[1,4,8192,3072]{3,2,1,0:T(8,128)(2,1)} %param.1, bf16[1,4,8192,1280]{3,2,1,0:T(8,128)(2,1)} %param), kind=kOutput, calls=%fused_computation.3 | convolution fusion | flops 257698037760 | bytes 348127232 | tf_op jit(solution)/rsntd,rsntf->rndf/dot_general | solution.py:10
  276.7 1205.6 %all-reduce.2 = bf16[1,4,1280,3072]{3,2,1,0:T(8,128)(2,1)} all-reduce(f32[1,4,1280,3072]{3,2,1,0:T(8,128)} %fusion.3), channel_id=1, replica_groups=[4,8]<=[32], use_global_device_ids=true, to_apply=%add.clone | all-reduce | flops 15728640 | bytes 94371840 | tf_op jit(solution)/rsntd,rsntf->rndf/dot_general | solution.py:10
where the time goes:
time: 1490 us; the launch traced here: 1480 us
  blocking collectives  1210 us (81%)
  matrix products  277 us (19%)
    dot_general x1, blocking collectives, step(): jnp.einsum('rsntd,rsntf->rndf', a, g, preferred_element_type=jnp.float32)  1210 us
    dot_general x1, matrix products, step(): jnp.einsum('rsntd,rsntf->rndf', a, g, preferred_element_type=jnp.float32)  277 us

commit v1 on v0

v1 whole, which is shorter than its diff:
```python
import functools

import jax
import jax.numpy as jnp
from jax import lax
from jax.experimental import pallas as pl
from jax.experimental.pallas import tpu as pltpu
from jax.sharding import PartitionSpec as P

MESH = pl.DeviceIdType.MESH
BM, BN = 640, 256
HALF, CH = BM // 2, BM // 4
ND, NP, NS, NT, NG, NF = 3, 8, 6, 4, 3, 4
DX, D1, D2, D3, D4 = 1, 3, 5, 7, 9


def kernel(dims, a, g, out, abuf, gbuf, acc, pend, dout, din, lsend, lrecv, psend, precv, tbuf,
           asem, gsem, d_s, d_r, l_s, l_r, p_s, p_r, t_sp, t_sl, t_sd, t_st, f_sl, f_sd, pt_r, lt_r, dt_r,
           cr_d, cr_l, cr_p):
    nm, K, M, N = dims
    I, J = M // BM, N // BN
    total = nm * I * J
    rep, dp = lax.axis_index("rep"), lax.axis_index("dp")
    z, c = dp // 2, lax.rem(dp, 2)
    sd = z // 2
    leaf = (z == 0) | (z == 3)
    inner = jnp.logical_not(leaf)
    rq, sq = sd, 1 - sd
    mate = (rep, z * 2 + 1 - c)
    near = (rep, jnp.where(leaf, 1 + sd, 3 * sd) * 2 + c)
    peer = (rep, (2 - sd) * 2 + c)

    bar = pltpu.get_barrier_semaphore()
    pl.semaphore_signal(bar, inc=1, device_id=mate, device_id_type=MESH)
    pl.semaphore_signal(bar, inc=1, device_id=near, device_id_type=MESH)

    @pl.when(inner)
    def _():
        pl.semaphore_signal(bar, inc=1, device_id=peer, device_id_type=MESH)

    def acopy(q, slot):
        n, i = q // I, lax.rem(q, I)
        return pltpu.make_async_copy(a.at[n, :, pl.ds(pl.multiple_of(i * BM, 128), BM)], abuf.at[slot], asem.at[slot])

    def gcopy(p, slot):
        n, j = p // (I * J), lax.rem(p, J)
        return pltpu.make_async_copy(g.at[n, :, pl.ds(pl.multiple_of(j * BN, 128), BN)], gbuf.at[slot], gsem.at[slot])

    acopy(0, 0).start()
    for p in range(NG - 1):
        gcopy(p, p).start()

    @pl.when(leaf)
    def _():
        pl.semaphore_wait(bar, 2)

    @pl.when(inner)
    def _():
        pl.semaphore_wait(bar, 3)

    def place(p, core, q):
        n, i, j = p // (I * J), lax.rem(p // J, I), lax.rem(p, J)
        row = i * BM + core * HALF + q * CH
        return out.at[n, pl.ds(pl.multiple_of(row, 32), CH), pl.ds(pl.multiple_of(j * BN, 128), BN)]

    def remote(src, dst, s, r, who):
        return pltpu.make_async_remote_copy(src, dst, s, r, device_id=who, device_id_type=MESH)

    def d_copy(p):
        return remote(dout.at[lax.rem(p, 2)], din.at[lax.rem(p, ND)], d_s.at[lax.rem(p, 2)], d_r.at[lax.rem(p, ND)], mate)

    def l_copy(p, q):
        s = lax.rem(p, NS)
        return remote(lsend.at[s, q], lrecv.at[s, q], l_s.at[s, q], l_r.at[s, q], near)

    def p_copy(p):
        s = lax.rem(p, NS)
        return remote(psend.at[s], precv.at[s], p_s.at[s], p_r.at[s], peer)

    def t_peer(p, q):
        s = lax.rem(p, NT)
        return remote(tbuf.at[s], place(p, c, q), t_sp.at[s], pt_r.at[p], peer)

    def t_leaf(p, q):
        s = lax.rem(p, NT)
        return remote(tbuf.at[s], place(p, c, q), t_sl.at[s], lt_r.at[p, 0], near)

    def t_mate(p, q):
        s = lax.rem(p, NT)
        return remote(tbuf.at[s], place(p, c, q), t_sd.at[s], dt_r.at[p, 0], mate)

    def t_own(p, q):
        s = lax.rem(p, NT)
        return pltpu.make_async_copy(tbuf.at[s], place(p, c, q), t_st.at[s])

    def f_leaf(p, q):
        return remote(place(p, c, q), place(p, c, q), f_sl.at[lax.rem(p, NF)], lt_r.at[p, 1], near)

    def f_mate(p, q, k):
        return remote(place(p, c, q), place(p, c, q), f_sd.at[lax.rem(p, NF), k], dt_r.at[p, k], mate)

    f32, bf16 = jnp.float32, jnp.bfloat16

    def compute(p):
        q = p // J
        qs, s = lax.rem(q, 2), lax.rem(p, NG)

        @pl.when(p + NG - 1 < total)
        def _():
            gcopy(p + NG - 1, lax.rem(p + NG - 1, NG)).start()

        @pl.when(lax.rem(p, J) == 0)
        def _():
            acopy(q, qs).wait()

            @pl.when(q + 1 < nm * I)
            def _():
                acopy(q + 1, 1 - qs).start()

        gcopy(p, s).wait()
        acc[...] = lax.dot_general(abuf[qs], gbuf[s], (((0,), (0,)), ((), ())), preferred_element_type=f32)

        @pl.when(p >= 2)
        def _():
            d_copy(p - 2).wait_send()

        ds, ps = lax.rem(p, 2), lax.rem(p, NP)
        for k in range(2):
            dout[ds, k] = acc[pl.ds(pl.multiple_of((1 - c) * HALF + k * CH, 32), CH), :].astype(bf16)

        @pl.when(p >= ND)
        def _():
            pl.semaphore_wait(cr_d, 1)

        d_copy(p).start()
        for k in range(2):
            pend[ps, k] = acc[pl.ds(pl.multiple_of(c * HALF + k * CH, 32), CH), :]

    def chip_sum(p):
        d_copy(p).wait_recv()
        ps, ds, ls = lax.rem(p, NP), lax.rem(p, ND), lax.rem(p, NS)

        @pl.when(leaf)
        def _():
            @pl.when(p >= NS)
            def _():
                pl.semaphore_wait(cr_l, 1)

            for q in (sq, rq):
                @pl.when(p >= NS)
                def _():
                    l_copy(p - NS, q).wait_send()

                lsend[ls, q] = (pend[ps, q] + din[ds, q].astype(f32)).astype(bf16)
                l_copy(p, q).start()

        @pl.when(inner)
        def _():
            for k in range(2):
                pend[ps, k] = pend[ps, k] + din[ds, k].astype(f32)

        @pl.when(p + ND < total)
        def _():
            pl.semaphore_signal(cr_d, inc=1, device_id=mate, device_id_type=MESH)

    def forward_partial(p):
        ps, s = lax.rem(p, NP), lax.rem(p, NS)
        l_copy(p, sq).wait_recv()

        @pl.when(p >= NS)
        def _():
            p_copy(p - NS).wait_send()
            pl.semaphore_wait(cr_p, 1)

        psend[s] = (pend[ps, sq] + lrecv[s, sq].astype(f32)).astype(bf16)
        p_copy(p).start()

    def finish(p):
        ps, s, t = lax.rem(p, NP), lax.rem(p, NS), lax.rem(p, NT)
        l_copy(p, rq).wait_recv()
        p_copy(p).wait_recv()

        @pl.when(p >= NT)
        def _():
            for f in (t_peer, t_leaf, t_mate):
                f(p - NT, rq).wait_send()
            t_own(p - NT, rq).wait()

        tbuf[t] = (pend[ps, rq] + lrecv[s, rq].astype(f32) + precv[s].astype(f32)).astype(bf16)
        t_peer(p, rq).start()
        t_leaf(p, rq).start()
        t_mate(p, rq).start()
        t_own(p, rq).start()

        @pl.when(p + NS < total)
        def _():
            pl.semaphore_signal(cr_l, inc=1, device_id=near, device_id_type=MESH)
            pl.semaphore_signal(cr_p, inc=1, device_id=peer, device_id_type=MESH)

    def pass_on(p):
        t_peer(p, sq).wait_recv()

        @pl.when(p >= NF)
        def _():
            f_leaf(p - NF, sq).wait_send()
            f_mate(p - NF, sq, 1).wait_send()

        f_leaf(p, sq).start()
        f_mate(p, sq, 1).start()

    def pass_leaf(p):
        t_leaf(p, rq).wait_recv()

        @pl.when(p >= NF)
        def _():
            f_mate(p - NF, rq, 0).wait_send()
            f_mate(p - NF, sq, 1).wait_send()

        f_mate(p, rq, 0).start()
        f_leaf(p, sq).wait_recv()
        f_mate(p, sq, 1).start()

    def within(e):
        return (e >= 0) & (e < total)

    def events(s):
        @pl.when(within(s - DX))
        def _():
            chip_sum(s - DX)

        @pl.when(inner)
        def _():
            @pl.when(within(s - D1))
            def _():
                forward_partial(s - D1)

            @pl.when(within(s - D2))
            def _():
                finish(s - D2)

            @pl.when(within(s - D3))
            def _():
                pass_on(s - D3)

        @pl.when(leaf & within(s - D4))
        def _():
            pass_leaf(s - D4)

    def step(s, _):
        compute(s)
        events(s)
        return 0

    lax.fori_loop(0, total, step, 0)

    def tail(s, _):
        events(s)
        return 0

    lax.fori_loop(total, total + max(D3, D4), tail, 0)

    for p in range(total - 2, total):
        d_copy(p).wait_send()

    def gone(lo, f):
        def body(p, _):
            f(p)
            return 0
        lax.fori_loop(lo, total, body, 0)

    @pl.when(leaf)
    def _():
        def f(p):
            l_copy(p, sq).wait_send()
            l_copy(p, rq).wait_send()
        gone(total - NS, f)

        def f(p):
            f_mate(p, rq, 0).wait_send()
            f_mate(p, sq, 1).wait_send()
        gone(total - NF, f)

    @pl.when(inner)
    def _():
        gone(total - NS, lambda p: p_copy(p).wait_send())

        def f(p):
            t_peer(p, rq).wait_send()
            t_leaf(p, rq).wait_send()
            t_mate(p, rq).wait_send()
            t_own(p, rq).wait()
        gone(total - NT, f)

        def f(p):
            f_leaf(p, sq).wait_send()
            f_mate(p, sq, 1).wait_send()
        gone(total - NF, f)

    def arrived(p):
        for k, q in ((0, rq), (1, sq)):
            where = place(p, 1 - c, q)
            remote(where, where, f_sd.at[0, 0], dt_r.at[p, k], mate).wait_recv()
    gone(0, arrived)


def solution(mesh):
    def step(a, g):
        _, nm, K, M = a.shape
        N = g.shape[-1]
        a, g = a.reshape(nm, K, M), g.reshape(nm, K, N)
        total = nm * (M // BM) * (N // BN)
        dma = pltpu.SemaphoreType.DMA
        bf16, f32 = jnp.bfloat16, jnp.float32
        return pl.pallas_call(
            functools.partial(kernel, (nm, K, M, N)),
            out_shape=jax.ShapeDtypeStruct((nm, M, N), bf16),
            in_specs=[pl.BlockSpec(memory_space=pl.ANY)] * 2,
            out_specs=pl.BlockSpec(memory_space=pl.ANY),
            scratch_shapes=[
                pltpu.VMEM((2, K, BM), bf16),
                pltpu.VMEM((NG, K, BN), bf16),
                pltpu.VMEM((BM, BN), f32),
                pltpu.VMEM((NP, 2, CH, BN), f32),
                pltpu.VMEM((2, 2, CH, BN), bf16),
                pltpu.VMEM((ND, 2, CH, BN), bf16),
                pltpu.VMEM((NS, 2, CH, BN), bf16),
                pltpu.VMEM((NS, 2, CH, BN), bf16),
                pltpu.VMEM((NS, CH, BN), bf16),
                pltpu.VMEM((NS, CH, BN), bf16),
                pltpu.VMEM((NT, CH, BN), bf16),
                dma((2,)), dma((NG,)), dma((2,)), dma((ND,)), dma((NS, 2)), dma((NS, 2)), dma((NS,)), dma((NS,)),
                dma((NT,)), dma((NT,)), dma((NT,)), dma((NT,)), dma((NF,)), dma((NF, 2)),
                dma((total,)), dma((total, 2)), dma((total, 2)),
                pltpu.SemaphoreType.REGULAR, pltpu.SemaphoreType.REGULAR, pltpu.SemaphoreType.REGULAR,
            ],
            compiler_params=pltpu.CompilerParams(
                collective_id=0, has_side_effects=True, vmem_limit_bytes=62 * 2**20
            ),
        )(a, g)

    return jax.shard_map(
        step,
        mesh=mesh,
        in_specs=(P(("rep", "dp"), None, None, None),) * 2,
        out_specs=P("rep", None, None),
        check_vma=False,
    )
```

time: 1490 us -> 396 us (0.27)
  blocking collectives: 1210 us -> 0 us
  Pallas kernels: 0 us -> 373 us
  matrix products: 277 us -> 0 us
  local copies, waits for them, and re-layouts: 0 us -> 21.5 us
    dot_general x1 -> x0, blocking collectives: 1210 us -> none  [step(): jnp.einsum('rsntd,rsntf->rndf', a, g, preferred_element_type=jnp.float32)]
    pallas_call x0 -> x1, Pallas kernels: none -> 373 us  [step(): pl.pallas_call(functools.partial(kernel, (nm, K, M, N)), out_shape=jax.Sh...]
    dot_general x1 -> x0, matrix products: 277 us -> none  [step(): jnp.einsum('rsntd,rsntf->rndf', a, g, preferred_element_type=jnp.float32)]
    unnamed x0 -> x1, local copies, waits for them, and re-layouts: none -> 21.5 us
where the time goes in v1:
time: 396 us; the launch traced here: 395 us
  Pallas kernels  373 us (94%)
  local copies, waits for them, and re-layouts  21.5 us (5%)
    pallas_call x1, Pallas kernels, step(): pl.pallas_call(functools.partial(kernel, (nm, K, M, N)), out_shape=jax.Sh...  373 us
    unnamed x1, local copies, waits for them, and re-layouts  21.5 us

profile of v1, /device:TPU:3, one launch (start us, length us, event | category | flops | bytes accessed | tf_op | source)
XLA Modules:
  0.0 394.6 jit_solution(7439802628428980757)
XLA Ops:
  0.0 373.1 %shard_map.28 = bf16[4,1280,3072]{2,1,0:T(8,128)(2,1)} custom-call(bf16[4,8192,1280]{2,1,0:T(8,128)(2,1)} %bitcast.a, bf16[4,8192,3072]{2,1,0:T(8,128)(2,1)} %bitcast.1.g), custom_call_target="tpu_custom_call" | custom-call | tf_op jit(solution)/shard_map/pallas_call | solution.py:314
  373.1 21.5 %copy.4 = bf16[4,1280,3072]{2,1,0:T(8,128)(2,1)} copy(bf16[4,1280,3072]{2,1,0:T(8,128)(2,1)} %shard_map.28) | data formatting | bytes 62914560

commit v2 on v0

v2 whole, which is shorter than its diff:
```python
import functools

import jax
import jax.numpy as jnp
from jax import lax
from jax.experimental import pallas as pl
from jax.experimental.pallas import tpu as pltpu
from jax.sharding import PartitionSpec as P

MESH = pl.DeviceIdType.MESH
BM, BN, KS = 640, 512, 4
U = 2
HALF, CH, CW = BM // 2, BM // 8, 2 * BN // U
WC = BN // CW
ND, NP, NS, NQ, NF = 2, 4, 4, 8, 8
RP, RL, RM = 8, 12, 7
OX, O1, O2, O3, O4, O5 = 1, 6, 9, 12, 18, 24
PUT = 4


def kernel(dims, a, g, out, abuf, gbuf, acc, pend, dout, din, lsend, lrecv, psend, precv,
           asem, gsem, d_s, d_r, l_s, l_r, p_s, p_r, t_sp, t_sl, f_sl, m_s, pt_r, lt_r, m_r,
           cr_d, cr_l, cr_p):
    nm, K, M, N = dims
    I, J, KC = M // BM, N // BN, K // KS
    total = nm * I * J
    units = U * total
    rep, dp = lax.axis_index("rep"), lax.axis_index("dp")
    z, c = dp // 2, lax.rem(dp, 2)
    sd = z // 2
    leaf = (z == 0) | (z == 3)
    inner = jnp.logical_not(leaf)
    rq, sq = sd, 1 - sd
    mate = (rep, z * 2 + 1 - c)
    near = (rep, jnp.where(leaf, 1 + sd, 3 * sd) * 2 + c)
    peer = (rep, (2 - sd) * 2 + c)
    f32, bf16 = jnp.float32, jnp.bfloat16

    bar = pltpu.get_barrier_semaphore()
    pl.semaphore_signal(bar, inc=1, device_id=mate, device_id_type=MESH)
    pl.semaphore_signal(bar, inc=1, device_id=near, device_id_type=MESH)

    @pl.when(inner)
    def _():
        pl.semaphore_signal(bar, inc=1, device_id=peer, device_id_type=MESH)

    def acopy(q, k):
        n, i = q // I, lax.rem(q, I)
        return pltpu.make_async_copy(
            a.at[n, pl.ds(k * KC, KC), pl.ds(pl.multiple_of(i * BM, 128), BM)], abuf.at[k], asem.at[k])

    def gcopy(p, k):
        n, j = p // (I * J), lax.rem(p, J)
        return pltpu.make_async_copy(
            g.at[n, pl.ds(k * KC, KC), pl.ds(pl.multiple_of(j * BN, 128), BN)], gbuf.at[k], gsem.at[k])

    for k in range(KS):
        acopy(0, k).start()
        gcopy(0, k).start()

    def start(p):
        n, i, j = p // (I * J), lax.rem(p // J, I), lax.rem(p, J)
        return n, i * BM, j * BN

    def place(u, q):
        n, row, col = start(u // U)
        row += c * HALF + (2 * q + lax.rem(u, U) // WC) * CH
        if WC > 1:
            col += lax.rem(u, WC) * CW
        return out.at[n, pl.ds(pl.multiple_of(row, 16), CH), pl.ds(pl.multiple_of(col, 128), CW)]

    def block(p, core, q):
        n, row, col = start(p)
        row += core * HALF + 2 * q * CH
        return out.at[n, pl.ds(pl.multiple_of(row, 16), 2 * CH), pl.ds(pl.multiple_of(col, 128), BN)]

    def remote(src, dst, s, r, who):
        return pltpu.make_async_remote_copy(src, dst, s, r, device_id=who, device_id_type=MESH)

    def d_copy(p):
        s = lax.rem(p, ND)
        return remote(dout.at[s], din.at[s], d_s.at[s], d_r.at[s], mate)

    def l_copy(u, q):
        s, h = lax.rem(u // U, NS), lax.rem(u, U)
        return remote(lsend.at[s, h, q], lrecv.at[s, h, q], l_s.at[s, h, q], l_r.at[s, h, q], near)

    def p_copy(u):
        s = lax.rem(u, NQ)
        return remote(psend.at[s], precv.at[s], p_s.at[s], p_r.at[s], peer)

    def t_peer(u, q):
        return remote(place(u, q), place(u, q), t_sp.at[lax.rem(u, NF)], pt_r.at[lax.rem(u, RP)], peer)

    def t_leaf(u, q):
        return remote(place(u, q), place(u, q), t_sl.at[lax.rem(u, NF)], lt_r.at[lax.rem(u, RL), 0], near)

    def f_leaf(u, q):
        return remote(place(u, q), place(u, q), f_sl.at[lax.rem(u, NF)], lt_r.at[lax.rem(u, RL), 1], near)

    def m_copy(p, q):
        return remote(block(p, c, q), block(p, c, q), m_s.at[lax.rem(p, 2), q], m_r.at[lax.rem(p, RM), q], mate)

    def to_mate(p, q):
        @pl.when(p >= 2)
        def _():
            m_copy(p - 2, q).wait_send()

        m_copy(p, q).start()

    def multiply(p, k):
        q, j = p // J, lax.rem(p, J)

        @pl.when(j == 0)
        def _():
            acopy(q, k).wait()

        gcopy(p, k).wait()
        d = lax.dot_general(abuf[k], gbuf[k], (((0,), (0,)), ((), ())), preferred_element_type=f32)
        if k == 0:
            acc[...] = d
        else:
            acc[...] += d

        @pl.when(p + 1 < total)
        def _():
            gcopy(p + 1, k).start()

            @pl.when(j == J - 1)
            def _():
                acopy(q + 1, k).start()

    def swap(p):
        s, ps = lax.rem(p, ND), lax.rem(p, NP)

        @pl.when(p >= ND)
        def _():
            d_copy(p - ND).wait_send()
            pl.semaphore_wait(cr_d, 1)

        def part(core, h, q):
            rows = pl.ds(pl.multiple_of(core * HALF + (2 * q + h // WC) * CH, 16), CH)
            cols = slice(h % WC * CW, (h % WC + 1) * CW)
            return acc[rows, cols]

        for h in range(U):
            for q in range(2):
                dout[s, h, q] = part(1 - c, h, q).astype(bf16)
        d_copy(p).start()
        for h in range(U):
            for q in range(2):
                pend[ps, h, q] = part(c, h, q)

    def chip_sum(p):
        d_copy(p).wait_recv()
        ps, ds, ls = lax.rem(p, NP), lax.rem(p, ND), lax.rem(p, NS)

        @pl.when(leaf)
        def _():
            @pl.when(p >= NS)
            def _():
                pl.semaphore_wait(cr_l, 1)

            for h in range(U):
                for q in (sq, rq):
                    @pl.when(p >= NS)
                    def _():
                        l_copy(U * (p - NS) + h, q).wait_send()

                    lsend[ls, h, q] = (pend[ps, h, q] + din[ds, h, q].astype(f32)).astype(bf16)
                    l_copy(U * p + h, q).start()

        @pl.when(inner)
        def _():
            for h in range(U):
                for q in range(2):
                    pend[ps, h, q] = pend[ps, h, q] + din[ds, h, q].astype(f32)

        @pl.when(p + ND < total)
        def _():
            pl.semaphore_signal(cr_d, inc=1, device_id=mate, device_id_type=MESH)

    def forward_partial(u):
        p, h, s = u // U, lax.rem(u, U), lax.rem(u, NQ)
        l_copy(u, sq).wait_recv()

        @pl.when(u >= NQ)
        def _():
            p_copy(u - NQ).wait_send()
            pl.semaphore_wait(cr_p, 1)

        psend[s] = (pend[lax.rem(p, NP), h, sq] + lrecv[lax.rem(p, NS), h, sq].astype(f32)).astype(bf16)
        p_copy(u).start()

    def finish(u):
        p, h, s = u // U, lax.rem(u, U), lax.rem(u, NQ)
        l_copy(u, rq).wait_recv()
        p_copy(u).wait_recv()

        @pl.when(u >= NF)
        def _():
            t_peer(u - NF, rq).wait_send()
            t_leaf(u - NF, rq).wait_send()

        where = place(u, rq)
        where[...] = (pend[lax.rem(p, NP), h, rq] + lrecv[lax.rem(p, NS), h, rq].astype(f32)
                      + precv[s].astype(f32)).astype(bf16)
        t_leaf(u, rq).start()
        t_peer(u, rq).start()

        @pl.when(u + NQ < units)
        def _():
            pl.semaphore_signal(cr_p, inc=1, device_id=peer, device_id_type=MESH)

        @pl.when(h == U - 1)
        def _():
            to_mate(p, rq)

            @pl.when(p + NS < total)
            def _():
                pl.semaphore_signal(cr_l, inc=1, device_id=near, device_id_type=MESH)

    def pass_on(u):
        t_peer(u, sq).wait_recv()

        @pl.when(u >= NF)
        def _():
            f_leaf(u - NF, sq).wait_send()

        f_leaf(u, sq).start()

        @pl.when(lax.rem(u, U) == U - 1)
        def _():
            to_mate(u // U, sq)

    def pass_leaf(u):
        t_leaf(u, rq).wait_recv()

        @pl.when(lax.rem(u, U) == U - 1)
        def _():
            to_mate(u // U, rq)

        f_leaf(u, sq).wait_recv()

        @pl.when(lax.rem(u, U) == U - 1)
        def _():
            to_mate(u // U, sq)

    def arrived(p):
        for q in range(2):
            where = block(p, 1 - c, q)
            remote(where, where, m_s.at[0, 0], m_r.at[lax.rem(p, RM), q], mate).wait_recv()

    def events(p, k):
        def due(lag, per, f):
            t = k - lag
            if t % per == 0:
                e = (4 // per) * p + t // per

                @pl.when((e >= 0) & (e < (4 // per) * total))
                def _():
                    f(e)

        due(3 + OX, 4, chip_sum)
        due(3 + O5, 4, arrived)

        @pl.when(inner)
        def _():
            due(O1, 4 // U, forward_partial)
            due(O2, 4 // U, finish)
            due(O3, 4 // U, pass_on)

        @pl.when(leaf)
        def _():
            due(O4, 4 // U, pass_leaf)

    def step(p, _):
        for k in range(KS):
            multiply(p, k)
            if k == 0:
                @pl.when(p == 0)
                def _():
                    pl.semaphore_wait(bar, jnp.where(leaf, 2, 3))
            if k == KS - 1:
                swap(p)
            events(p, k)
        return 0

    lax.fori_loop(0, total, step, 0)

    def tail(p, _):
        for k in range(KS):
            events(p, k)
        return 0

    lax.fori_loop(total, total + (O5 + 3) // 4 + 1, tail, 0)

    def gone(lo, hi, f):
        def body(p, _):
            f(p)
            return 0
        lax.fori_loop(lo, hi, body, 0)

    gone(total - ND, total, lambda p: d_copy(p).wait_send())

    def f(p):
        m_copy(p, rq).wait_send()
        m_copy(p, sq).wait_send()
    gone(total - 2, total, f)

    @pl.when(leaf)
    def _():
        def f(u):
            l_copy(u, sq).wait_send()
            l_copy(u, rq).wait_send()
        gone(units - U * NS, units, f)

    @pl.when(inner)
    def _():
        gone(units - NQ, units, lambda u: p_copy(u).wait_send())

        def f(u):
            t_peer(u, rq).wait_send()
            t_leaf(u, rq).wait_send()
            f_leaf(u, sq).wait_send()
        gone(units - NF, units, f)


def put(x, out, sems):
    rows = x.shape[1] // PUT
    copies = [
        pltpu.make_async_copy(x.at[n, pl.ds(r * rows, rows)], out.at[n, pl.ds(r * rows, rows)], sems.at[n, r])
        for n in range(x.shape[0]) for r in range(PUT)
    ]
    for one in copies:
        one.start()
    for one in copies:
        one.wait()


def solution(mesh):
    def step(a, g):
        _, nm, K, M = a.shape
        N = g.shape[-1]
        a, g = a.reshape(nm, K, M), g.reshape(nm, K, N)
        total = nm * (M // BM) * (N // BN)
        dma = pltpu.SemaphoreType.DMA
        bf16, f32 = jnp.bfloat16, jnp.float32
        sums = pl.pallas_call(
            functools.partial(kernel, (nm, K, M, N)),
            out_shape=pltpu.VMEM((nm, M, N), bf16),
            in_specs=[pl.BlockSpec(memory_space=pl.ANY)] * 2,
            out_specs=pl.BlockSpec(memory_space=pltpu.VMEM),
            scratch_shapes=[
                pltpu.VMEM((KS, K // KS, BM), bf16),
                pltpu.VMEM((KS, K // KS, BN), bf16),
                pltpu.VMEM((BM, BN), f32),
                pltpu.VMEM((NP, U, 2, CH, CW), f32),
                pltpu.VMEM((ND, U, 2, CH, CW), bf16),
                pltpu.VMEM((ND, U, 2, CH, CW), bf16),
                pltpu.VMEM((NS, U, 2, CH, CW), bf16),
                pltpu.VMEM((NS, U, 2, CH, CW), bf16),
                pltpu.VMEM((NQ, CH, CW), bf16),
                pltpu.VMEM((NQ, CH, CW), bf16),
                dma((KS,)), dma((KS,)), dma((ND,)), dma((ND,)), dma((NS, U, 2)), dma((NS, U, 2)),
                dma((NQ,)), dma((NQ,)), dma((NF,)), dma((NF,)), dma((NF,)), dma((2, 2)),
                dma((RP,)), dma((RL, 2)), dma((RM, 2)),
                pltpu.SemaphoreType.REGULAR, pltpu.SemaphoreType.REGULAR, pltpu.SemaphoreType.REGULAR,
            ],
            compiler_params=pltpu.CompilerParams(
                collective_id=0, has_side_effects=True, vmem_limit_bytes=33 * 2**20
            ),
        )(a, g)
        return pl.pallas_call(
            put,
            out_shape=jax.ShapeDtypeStruct((nm, M, N), bf16),
            in_specs=[pl.BlockSpec(memory_space=pltpu.VMEM)],
            out_specs=pl.BlockSpec(memory_space=pl.ANY),
            scratch_shapes=[dma((nm, PUT))],
            compiler_params=pltpu.CompilerParams(vmem_limit_bytes=2**20),
        )(sums)

    return jax.shard_map(
        step,
        mesh=mesh,
        in_specs=(P(("rep", "dp"), None, None, None),) * 2,
        out_specs=P("rep", None, None),
        check_vma=False,
    )
```

time: 1490 us -> 375 us (0.25)
  blocking collectives: 1210 us -> 0 us
  Pallas kernels: 0 us -> 374 us
  matrix products: 277 us -> 0 us
    dot_general x1 -> x0, blocking collectives: 1210 us -> none  [step(): jnp.einsum('rsntd,rsntf->rndf', a, g, preferred_element_type=jnp.float32)]
    pallas_call x0 -> x2, Pallas kernels: none -> 374 us  [the longest x1 364 us: step(): pl.pallas_call(functools.partial(kernel, (nm, K, M, N)), out_shape=pltpu....]
    dot_general x1 -> x0, matrix products: 277 us -> none  [step(): jnp.einsum('rsntd,rsntf->rndf', a, g, preferred_element_type=jnp.float32)]
where the time goes in v2:
time: 375 us; the launch traced here: 374 us
  Pallas kernels  374 us (100%)
    pallas_call x1, Pallas kernels, step(): pl.pallas_call(functools.partial(kernel, (nm, K, M, N)), out_shape=pltpu....  364 us
    pallas_call x1, Pallas kernels, step(): pl.pallas_call(put, out_shape=jax.ShapeDtypeStruct((nm, M, N), bf16), in_...  10.4 us

profile of v2, /device:TPU:3, one launch (start us, length us, event | category | flops | bytes accessed | tf_op | source)
XLA Modules:
  0.0 374.0 jit_solution(8785171177544082897)
XLA Ops:
  0.0 363.5 %shard_map.28.x = bf16[4,1280,3072]{2,1,0:T(8,128)(2,1)S(1)} custom-call(bf16[4,8192,1280]{2,1,0:T(8,128)(2,1)} %bitcast.a, bf16[4,8192,3072]{2,1,0:T(8,128)(2,1)} %bitcast.1.g), custom_call_target="tpu_custom_call" | custom-call | tf_op jit(solution)/shard_map/pallas_call | solution.py:349
  363.5 10.4 %shard_map.29 = bf16[4,1280,3072]{2,1,0:T(8,128)(2,1)} custom-call(bf16[4,1280,3072]{2,1,0:T(8,128)(2,1)S(1)} %shard_map.28.x), custom_call_target="tpu_custom_call" | custom-call | tf_op jit(solution)/shard_map/pallas_call | solution.py:374

commit v3 on v0

v3 whole, which is shorter than its diff:
```python
import functools

import jax
import jax.numpy as jnp
from jax import lax
from jax.experimental import pallas as pl
from jax.experimental.pallas import tpu as pltpu
from jax.sharding import PartitionSpec as P

MESH = pl.DeviceIdType.MESH
BM, BN, KS = 640, 512, 4
U = 2
HALF, CH, CW = BM // 2, BM // 8, 2 * BN // U
WC = BN // CW
ND, NP, NS, NR, NF = 2, 4, 4, 2, 2
RP, RL, RM = 3, 4, 7
SUM, HELD = 4, 25
PARTIAL = 5, 5
FINISH = 9, 6
PASS = 10, 11
LEAF = 19
HEAD = 10
PUT = 4


def kernel(dims, a, g, out, abuf, gbuf, acc, pend, dout, din, lsend, lrecv, psend, precv,
           asem, gsem, d_s, d_r, l_s, l_r, p_s, p_r, t_sp, t_sl, f_sl, m_s, pt_r, lt_r, m_r,
           cr_d, cr_l, cr_p):
    nm, K, M, N = dims
    I, J, KC = M // BM, N // BN, K // KS
    total = nm * I * J
    rep, dp = lax.axis_index("rep"), lax.axis_index("dp")
    z, c = lax.div(dp, 2), lax.rem(dp, 2)
    sd = lax.div(z, 2)
    leaf = (z == 0) | (z == 3)
    inner = jnp.logical_not(leaf)
    rq, sq = sd, 1 - sd
    mate = (rep, z * 2 + 1 - c)
    near = (rep, jnp.where(leaf, 1 + sd, 3 * sd) * 2 + c)
    peer = (rep, (2 - sd) * 2 + c)
    f32, bf16 = jnp.float32, jnp.bfloat16

    bar = pltpu.get_barrier_semaphore()
    pl.semaphore_signal(bar, inc=1, device_id=mate, device_id_type=MESH)
    pl.semaphore_signal(bar, inc=1, device_id=near, device_id_type=MESH)

    @pl.when(inner)
    def _():
        pl.semaphore_signal(bar, inc=1, device_id=peer, device_id_type=MESH)

    def start(p):
        n, i, j = lax.div(p, I * J), lax.rem(lax.div(p, J), I), lax.rem(p, J)
        return n, i * BM, j * BN

    def acopy(q, k):
        n, i = lax.div(q, I), lax.rem(q, I)
        return pltpu.make_async_copy(
            a.at[n, pl.ds(k * KC, KC), pl.ds(pl.multiple_of(i * BM, 128), BM)], abuf.at[k], asem.at[k])

    def gcopy(p, k):
        n, _, col = start(p)
        return pltpu.make_async_copy(
            g.at[n, pl.ds(k * KC, KC), pl.ds(pl.multiple_of(col, 128), BN)], gbuf.at[k], gsem.at[k])

    for k in range(KS):
        acopy(0, k).start()
        gcopy(0, k).start()

    def remote(src, dst, s, r, who):
        return pltpu.make_async_remote_copy(src, dst, s, r, device_id=who, device_id_type=MESH)

    class Piece:
        def __init__(self, p, sure, place=None):
            self.p, self.sure, self.place = p, sure, place or start(p)

        def slot(self, n):
            return lax.rem(self.p, n)

        def half(self, core):
            n, row, col = self.place
            row = row + core * HALF
            return out.at[n, pl.ds(pl.multiple_of(row, 16), HALF), pl.ds(pl.multiple_of(col, 128), BN)]

        def block(self, core, q):
            n, row, col = self.place
            row = row + core * HALF + 2 * q * CH
            return out.at[n, pl.ds(pl.multiple_of(row, 16), 2 * CH), pl.ds(pl.multiple_of(col, 128), BN)]

        def message(self, q, h):
            n, row, col = self.place
            row, col = row + c * HALF + (2 * q + h // WC) * CH, col + h % WC * CW
            return out.at[n, pl.ds(pl.multiple_of(row, 16), CH), pl.ds(pl.multiple_of(col, 128), CW)]

        def d_copy(self):
            s = self.slot(ND)
            return remote(dout.at[s], din.at[s], d_s.at[s], d_r.at[s], mate)

        def l_copy(self, h, q):
            s = self.slot(NS)
            return remote(lsend.at[s, h, q], lrecv.at[s, h, q], l_s.at[s], l_r.at[s, h, q], near)

        def p_copy(self, h):
            s = self.slot(NR)
            return remote(psend.at[s, h], precv.at[s, h], p_s.at[s], p_r.at[s, h], peer)

        def t_peer(self, h, q):
            at = self.message(q, h)
            return remote(at, at, t_sp.at[self.slot(NF)], pt_r.at[self.slot(RP), h], peer)

        def t_leaf(self, h, q):
            at = self.message(q, h)
            return remote(at, at, t_sl.at[self.slot(NF)], lt_r.at[self.slot(RL)], near)

        def f_leaf(self, h, q):
            at = self.message(q, h)
            return remote(at, at, f_sl.at[self.slot(NF)], lt_r.at[self.slot(RL)], near)

        def m_copy(self, q):
            at = self.block(c, q)
            return remote(at, at, m_s.at[self.slot(2)], m_r.at[self.slot(RM)], mate)

        def l_sent(self):
            s = self.slot(NS)
            remote(lsend.at[s], lrecv.at[s], l_s.at[s], l_r.at[s, 0, 0], near).wait_send()

        def p_sent(self):
            s = self.slot(NR)
            remote(psend.at[s], precv.at[s], p_s.at[s], p_r.at[s, 0], peer).wait_send()

        def t_sent(self):
            s, at = self.slot(NF), self.block(c, rq)
            remote(at, at, t_sp.at[s], pt_r.at[0, 0], peer).wait_send()
            remote(at, at, t_sl.at[s], lt_r.at[0], near).wait_send()

        def f_sent(self):
            at = self.block(c, sq)
            remote(at, at, f_sl.at[self.slot(NF)], lt_r.at[0], near).wait_send()

        def m_sent(self):
            at = self.half(c)
            remote(at, at, m_s.at[self.slot(2)], m_r.at[0], mate).wait_send()

        def whole(self):
            at = self.half(c)
            remote(at, at, t_sl.at[0], lt_r.at[self.slot(RL)], near).wait_recv()

        def given(self):
            at = self.half(1 - c)
            remote(at, at, m_s.at[0], m_r.at[self.slot(RM)], mate).wait_recv()

    def multiply(p, k):
        q, j = lax.div(p, J), lax.rem(p, J)

        @pl.when(j == 0)
        def _():
            acopy(q, k).wait()

        gcopy(p, k).wait()
        d = lax.dot_general(abuf[k], gbuf[k], (((0,), (0,)), ((), ())), preferred_element_type=f32)
        if k == 0:
            acc[...] = d
        else:
            acc[...] += d

        @pl.when(p + 1 < total)
        def _():
            gcopy(p + 1, k).start()

            @pl.when(j == J - 1)
            def _():
                acopy(q + 1, k).start()

    def again(it, n, f):
        if it.sure:
            f()
        else:
            pl.when(it.p >= n)(f)

    def swap(it):
        s, ps = it.slot(ND), it.slot(NP)

        def free():
            it.d_copy().wait_send()
            pl.semaphore_wait(cr_d, 1)
        again(it, ND, free)

        def part(core, h, q):
            rows = pl.ds(pl.multiple_of(core * HALF + (2 * q + h // WC) * CH, 16), CH)
            return acc[rows, h % WC * CW:(h % WC + 1) * CW]

        for h in range(U):
            for q in range(2):
                dout[s, h, q] = part(1 - c, h, q).astype(bf16)
        it.d_copy().start()
        for h in range(U):
            for q in range(2):
                pend[ps, h, q] = part(c, h, q)

    def chip_sum(it):
        it.d_copy().wait_recv()
        ps, ds, ls = it.slot(NP), it.slot(ND), it.slot(NS)

        @pl.when(leaf)
        def _():
            def free():
                pl.semaphore_wait(cr_l, 1)
                it.l_sent()
            again(it, NS, free)
            for h in range(U):
                for q in (sq, rq):
                    lsend[ls, h, q] = (pend[ps, h, q] + din[ds, h, q].astype(f32)).astype(bf16)
                    it.l_copy(h, q).start()

        @pl.when(inner)
        def _():
            for h in range(U):
                for q in range(2):
                    pend[ps, h, q] = pend[ps, h, q] + din[ds, h, q].astype(f32)

        pl.semaphore_signal(cr_d, inc=1, device_id=mate, device_id_type=MESH)

    def forward_partial(it, h):
        it.l_copy(h, sq).wait_recv()
        if h == 0:
            again(it, NR, it.p_sent)
        again(it, NR, lambda: pl.semaphore_wait(cr_p, 1))
        psend[it.slot(NR), h] = (pend[it.slot(NP), h, sq] + lrecv[it.slot(NS), h, sq].astype(f32)).astype(bf16)
        it.p_copy(h).start()

    def finish(it, h):
        it.l_copy(h, rq).wait_recv()
        it.p_copy(h).wait_recv()
        if h == 0:
            again(it, NF, it.t_sent)
        where = it.message(rq, h)
        where[...] = (pend[it.slot(NP), h, rq] + lrecv[it.slot(NS), h, rq].astype(f32)
                      + precv[it.slot(NR), h].astype(f32)).astype(bf16)
        it.t_leaf(h, rq).start()
        it.t_peer(h, rq).start()
        pl.semaphore_signal(cr_p, inc=1, device_id=peer, device_id_type=MESH)
        if h == U - 1:
            again(it, 2, it.m_sent)
            it.m_copy(rq).start()
            pl.semaphore_signal(cr_l, inc=1, device_id=near, device_id_type=MESH)

    def pass_on(it, h):
        it.t_peer(h, sq).wait_recv()
        if h == 0:
            again(it, NF, it.f_sent)
        it.f_leaf(h, sq).start()
        if h == U - 1:
            it.m_copy(sq).start()

    def pass_leaf(it):
        it.whole()
        again(it, 2, it.m_sent)
        it.m_copy(rq).start()
        it.m_copy(sq).start()

    def arrived(it):
        it.given()

    def events(pieces, k, phase):
        def due(lag, f, *h):
            if (k - lag) % 4:
                return
            it = pieces[(lag - k) // 4]
            if phase == "body":
                f(it, *h)
            else:
                pl.when(it.p >= 0 if phase == "head" else it.p < total)(lambda: f(it, *h))

        def inners(side):
            for lags, f in ((PARTIAL, forward_partial), (FINISH, finish), (PASS, pass_on)):
                for h in range(U):
                    due(lags[side] + 4 // U * h, f, h)

        for side in range(2):
            pl.when(inner & (sd == side))(functools.partial(inners, side))
        due(SUM, chip_sum)

        @pl.when(leaf)
        def _():
            due(LEAF, pass_leaf)

        due(HELD, arrived)

    def recent(p, phase):
        return [Piece(p - n, phase != "head") for n in range(HELD // 4 + 1)]

    def step(phase, p, _):
        pieces = recent(p, phase)
        for k in range(KS):
            multiply(p, k)
            if k == 0 and phase == "head":
                @pl.when(p == 0)
                def _():
                    pl.semaphore_wait(bar, jnp.where(leaf, 2, 3))
            if k == KS - 1:
                swap(pieces[0])
            events(pieces, k, phase)
        return 0

    lax.fori_loop(0, HEAD, functools.partial(step, "head"), 0)
    lax.fori_loop(HEAD, total, functools.partial(step, "body"), 0)

    def tail(p, _):
        pieces = recent(p, "tail")
        for k in range(KS):
            events(pieces, k, "tail")
        return 0

    last = total + HELD // 4 + 1
    lax.fori_loop(total, last - 2, tail, 0)

    def gone(n, f):
        def body(p, _):
            f(Piece(p, True))
            return 0
        lax.fori_loop(total - n, total, body, 0)

    pl.semaphore_wait(cr_d, ND)
    gone(ND, lambda it: it.d_copy().wait_send())

    @pl.when(leaf)
    def _():
        pl.semaphore_wait(cr_l, NS)
        gone(NS, Piece.l_sent)

    @pl.when(inner)
    def _():
        pl.semaphore_wait(cr_p, NR * U)
        gone(NR, Piece.p_sent)
        gone(NF, Piece.t_sent)
        gone(NF, Piece.f_sent)

    lax.fori_loop(last - 2, last, tail, 0)

    gone(2, Piece.m_sent)


def put(x, out, sems):
    rows = x.shape[1] // PUT
    copies = [
        pltpu.make_async_copy(x.at[n, pl.ds(r * rows, rows)], out.at[n, pl.ds(r * rows, rows)], sems.at[n, r])
        for n in range(x.shape[0]) for r in range(PUT)
    ]
    for one in copies:
        one.start()
    for one in copies:
        one.wait()


def solution(mesh):
    def step(a, g):
        _, nm, K, M = a.shape
        N = g.shape[-1]
        a, g = a.reshape(nm, K, M), g.reshape(nm, K, N)
        dma = pltpu.SemaphoreType.DMA
        bf16, f32 = jnp.bfloat16, jnp.float32
        sums = pl.pallas_call(
            functools.partial(kernel, (nm, K, M, N)),
            out_shape=pltpu.VMEM((nm, M, N), bf16),
            in_specs=[pl.BlockSpec(memory_space=pl.ANY)] * 2,
            out_specs=pl.BlockSpec(memory_space=pltpu.VMEM),
            scratch_shapes=[
                pltpu.VMEM((KS, K // KS, BM), bf16),
                pltpu.VMEM((KS, K // KS, BN), bf16),
                pltpu.VMEM((BM, BN), f32),
                pltpu.VMEM((NP, U, 2, CH, CW), f32),
                pltpu.VMEM((ND, U, 2, CH, CW), bf16),
                pltpu.VMEM((ND, U, 2, CH, CW), bf16),
                pltpu.VMEM((NS, U, 2, CH, CW), bf16),
                pltpu.VMEM((NS, U, 2, CH, CW), bf16),
                pltpu.VMEM((NR, U, CH, CW), bf16),
                pltpu.VMEM((NR, U, CH, CW), bf16),
                dma((KS,)), dma((KS,)), dma((ND,)), dma((ND,)), dma((NS,)), dma((NS, U, 2)),
                dma((NR,)), dma((NR, U)), dma((NF,)), dma((NF,)), dma((NF,)), dma((2,)),
                dma((RP, U)), dma((RL,)), dma((RM,)),
                pltpu.SemaphoreType.REGULAR, pltpu.SemaphoreType.REGULAR, pltpu.SemaphoreType.REGULAR,
            ],
            compiler_params=pltpu.CompilerParams(
                collective_id=0, has_side_effects=True, vmem_limit_bytes=33 * 2**20
            ),
        )(a, g)
        return pl.pallas_call(
            put,
            out_shape=jax.ShapeDtypeStruct((nm, M, N), bf16),
            in_specs=[pl.BlockSpec(memory_space=pltpu.VMEM)],
            out_specs=pl.BlockSpec(memory_space=pl.ANY),
            scratch_shapes=[dma((nm, PUT))],
            compiler_params=pltpu.CompilerParams(vmem_limit_bytes=2**20),
        )(sums)

    return jax.shard_map(
        step,
        mesh=mesh,
        in_specs=(P(("rep", "dp"), None, None, None),) * 2,
        out_specs=P("rep", None, None),
        check_vma=False,
    )
```

time: 1490 us -> 373 us (0.25)
  blocking collectives: 1210 us -> 0 us
  Pallas kernels: 0 us -> 373 us
  matrix products: 277 us -> 0 us
    dot_general x1 -> x0, blocking collectives: 1210 us -> none  [step(): jnp.einsum('rsntd,rsntf->rndf', a, g, preferred_element_type=jnp.float32)]
    pallas_call x0 -> x2, Pallas kernels: none -> 373 us  [the longest x1 363 us: step(): pl.pallas_call(functools.partial(kernel, (nm, K, M, N)), out_shape=pltpu....]
    dot_general x1 -> x0, matrix products: 277 us -> none  [step(): jnp.einsum('rsntd,rsntf->rndf', a, g, preferred_element_type=jnp.float32)]
where the time goes in v3:
time: 373 us
  Pallas kernels  373 us (100%)
    pallas_call x1, Pallas kernels, step(): pl.pallas_call(functools.partial(kernel, (nm, K, M, N)), out_shape=pltpu....  363 us
    pallas_call x1, Pallas kernels, step(): pl.pallas_call(put, out_shape=jax.ShapeDtypeStruct((nm, M, N), bf16), in_...  10.4 us

profile of v3, /device:TPU:3, one launch (start us, length us, event | category | flops | bytes accessed | tf_op | source)
XLA Modules:
  0.0 373.1 jit_solution(5753667204594541635)
XLA Ops:
  0.0 362.7 %shard_map.28.x = bf16[4,1280,3072]{2,1,0:T(8,128)(2,1)S(1)} custom-call(bf16[4,8192,1280]{2,1,0:T(8,128)(2,1)} %bitcast.a, bf16[4,8192,3072]{2,1,0:T(8,128)(2,1)} %bitcast.1.g), custom_call_target="tpu_custom_call" | custom-call | tf_op jit(solution)/shard_map/pallas_call | solution.py:361
  362.7 10.4 %shard_map.29 = bf16[4,1280,3072]{2,1,0:T(8,128)(2,1)} custom-call(bf16[4,1280,3072]{2,1,0:T(8,128)(2,1)S(1)} %shard_map.28.x), custom_call_target="tpu_custom_call" | custom-call | tf_op jit(solution)/shard_map/pallas_call | solution.py:386

commit v4 on v3

--- a/solution.py
+++ b/solution.py
@@ -9,6 +9,7 @@
 
 MESH = pl.DeviceIdType.MESH
 BM, BN, KS = 640, 512, 4
+FIRST = 2
 U = 2
 HALF, CH, CW = BM // 2, BM // 8, 2 * BN // U
 WC = BN // CW
@@ -21,6 +22,18 @@
 LEAF = 19
 HEAD = 10
 PUT = 4
+
+
+def div(x, n):
+    return x // n if isinstance(x, int) else lax.div(x, n)
+
+
+def rem(x, n):
+    return x % n if isinstance(x, int) else lax.rem(x, n)
+
+
+def whole_of(x, n):
+    return x if isinstance(x, int) else pl.multiple_of(x, n)
 
 
 def kernel(dims, a, g, out, abuf, gbuf, acc, pend, dout, din, lsend, lrecv, psend, precv,
@@ -49,22 +62,35 @@
         pl.semaphore_signal(bar, inc=1, device_id=peer, device_id_type=MESH)
 
     def start(p):
-        n, i, j = lax.div(p, I * J), lax.rem(lax.div(p, J), I), lax.rem(p, J)
+        n, i, j = div(p, I * J), rem(div(p, J), I), rem(p, J)
         return n, i * BM, j * BN
 
     def acopy(q, k):
-        n, i = lax.div(q, I), lax.rem(q, I)
+        n, i = div(q, I), rem(q, I)
         return pltpu.make_async_copy(
-            a.at[n, pl.ds(k * KC, KC), pl.ds(pl.multiple_of(i * BM, 128), BM)], abuf.at[k], asem.at[k])
+            a.at[n, pl.ds(k * KC, KC), pl.ds(whole_of(i * BM, 128), BM)], abuf.at[k], asem.at[k])
 
     def gcopy(p, k):
         n, _, col = start(p)
         return pltpu.make_async_copy(
-            g.at[n, pl.ds(k * KC, KC), pl.ds(pl.multiple_of(col, 128), BN)], gbuf.at[k], gsem.at[k])
+            g.at[n, pl.ds(k * KC, KC), pl.ds(whole_of(col, 128), BN)], gbuf.at[k], gsem.at[k])
+
+    KF = KC // FIRST
+
+    def afirst(k, f):
+        rows = pl.ds(k * KC + f * KF, KF)
+        return pltpu.make_async_copy(
+            a.at[0, rows, pl.ds(0, BM)], abuf.at[k, pl.ds(f * KF, KF)], asem.at[k + f * KS])
+
+    def gfirst(k, f):
+        rows = pl.ds(k * KC + f * KF, KF)
+        return pltpu.make_async_copy(
+            g.at[0, rows, pl.ds(0, BN)], gbuf.at[k, pl.ds(f * KF, KF)], gsem.at[k + f * KS])
 
     for k in range(KS):
-        acopy(0, k).start()
-        gcopy(0, k).start()
+        for f in range(FIRST):
+            afirst(k, f).start()
+            gfirst(k, f).start()
 
     def remote(src, dst, s, r, who):
         return pltpu.make_async_remote_copy(src, dst, s, r, device_id=who, device_id_type=MESH)
@@ -74,22 +100,22 @@
             self.p, self.sure, self.place = p, sure, place or start(p)
 
         def slot(self, n):
-            return lax.rem(self.p, n)
+            return rem(self.p, n)
 
         def half(self, core):
             n, row, col = self.place
             row = row + core * HALF
-            return out.at[n, pl.ds(pl.multiple_of(row, 16), HALF), pl.ds(pl.multiple_of(col, 128), BN)]
+            return out.at[n, pl.ds(whole_of(row, 16), HALF), pl.ds(whole_of(col, 128), BN)]
 
         def block(self, core, q):
             n, row, col = self.place
             row = row + core * HALF + 2 * q * CH
-            return out.at[n, pl.ds(pl.multiple_of(row, 16), 2 * CH), pl.ds(pl.multiple_of(col, 128), BN)]
+            return out.at[n, pl.ds(whole_of(row, 16), 2 * CH), pl.ds(whole_of(col, 128), BN)]
 
         def message(self, q, h):
             n, row, col = self.place
             row, col = row + c * HALF + (2 * q + h // WC) * CH, col + h % WC * CW
-            return out.at[n, pl.ds(pl.multiple_of(row, 16), CH), pl.ds(pl.multiple_of(col, 128), CW)]
+            return out.at[n, pl.ds(whole_of(row, 16), CH), pl.ds(whole_of(col, 128), CW)]
 
         def d_copy(self):
             s = self.slot(ND)
@@ -109,11 +135,11 @@
 
         def t_leaf(self, h, q):
             at = self.message(q, h)
-            return remote(at, at, t_sl.at[self.slot(NF)], lt_r.at[self.slot(RL)], near)
+            return remote(at, at, t_sl.at[self.slot(NF)], lt_r.at[self.slot(RL), 0], near)
 
         def f_leaf(self, h, q):
             at = self.message(q, h)
-            return remote(at, at, f_sl.at[self.slot(NF)], lt_r.at[self.slot(RL)], near)
+            return remote(at, at, f_sl.at[self.slot(NF)], lt_r.at[self.slot(RL), 1], near)
 
         def m_copy(self, q):
             at = self.block(c, q)
@@ -130,26 +156,26 @@
         def t_sent(self):
             s, at = self.slot(NF), self.block(c, rq)
             remote(at, at, t_sp.at[s], pt_r.at[0, 0], peer).wait_send()
-            remote(at, at, t_sl.at[s], lt_r.at[0], near).wait_send()
+            remote(at, at, t_sl.at[s], lt_r.at[0, 0], near).wait_send()
 
         def f_sent(self):
             at = self.block(c, sq)
-            remote(at, at, f_sl.at[self.slot(NF)], lt_r.at[0], near).wait_send()
+            remote(at, at, f_sl.at[self.slot(NF)], lt_r.at[0, 0], near).wait_send()
 
         def m_sent(self):
             at = self.half(c)
             remote(at, at, m_s.at[self.slot(2)], m_r.at[0], mate).wait_send()
 
-        def whole(self):
-            at = self.half(c)
-            remote(at, at, t_sl.at[0], lt_r.at[self.slot(RL)], near).wait_recv()
+        def whole(self, k, q):
+            at = self.block(c, q)
+            remote(at, at, t_sl.at[0], lt_r.at[self.slot(RL), k], near).wait_recv()
 
         def given(self):
             at = self.half(1 - c)
             remote(at, at, m_s.at[0], m_r.at[self.slot(RM)], mate).wait_recv()
 
     def multiply(p, k):
-        q, j = lax.div(p, J), lax.rem(p, J)
+        q, j = div(p, J), rem(p, J)
 
         @pl.when(j == 0)
         def _():
@@ -252,9 +278,10 @@
             it.m_copy(sq).start()
 
     def pass_leaf(it):
-        it.whole()
+        it.whole(0, rq)
         again(it, 2, it.m_sent)
         it.m_copy(rq).start()
+        it.whole(1, sq)
         it.m_copy(sq).start()
 
     def arrived(it):
@@ -267,7 +294,7 @@
             it = pieces[(lag - k) // 4]
             if phase == "body":
                 f(it, *h)
-            else:
+            elif phase == "head" or phase == "tail":
                 pl.when(it.p >= 0 if phase == "head" else it.p < total)(lambda: f(it, *h))
 
         def inners(side):
@@ -292,16 +319,27 @@
         pieces = recent(p, phase)
         for k in range(KS):
             multiply(p, k)
-            if k == 0 and phase == "head":
-                @pl.when(p == 0)
-                def _():
-                    pl.semaphore_wait(bar, jnp.where(leaf, 2, 3))
             if k == KS - 1:
                 swap(pieces[0])
             events(pieces, k, phase)
         return 0
 
-    lax.fori_loop(0, HEAD, functools.partial(step, "head"), 0)
+    for k in range(KS):
+        for f in range(FIRST):
+            afirst(k, f).wait()
+            gfirst(k, f).wait()
+            rows = slice(f * KF, (f + 1) * KF)
+            d = lax.dot_general(
+                abuf[k, rows], gbuf[k, rows], (((0,), (0,)), ((), ())), preferred_element_type=f32)
+            if k + f == 0:
+                acc[...] = d
+            else:
+                acc[...] += d
+        gcopy(1, k).start()
+    pl.semaphore_wait(bar, jnp.where(leaf, 2, 3))
+    swap(Piece(0, False))
+
+    lax.fori_loop(1, HEAD, functools.partial(step, "head"), 0)
     lax.fori_loop(HEAD, total, functools.partial(step, "body"), 0)
 
     def tail(p, _):
@@ -374,9 +412,9 @@
                 pltpu.VMEM((NS, U, 2, CH, CW), bf16),
                 pltpu.VMEM((NR, U, CH, CW), bf16),
                 pltpu.VMEM((NR, U, CH, CW), bf16),
-                dma((KS,)), dma((KS,)), dma((ND,)), dma((ND,)), dma((NS,)), dma((NS, U, 2)),
+                dma((KS * FIRST,)), dma((KS * FIRST,)), dma((ND,)), dma((ND,)), dma((NS,)), dma((NS, U, 2)),
                 dma((NR,)), dma((NR, U)), dma((NF,)), dma((NF,)), dma((NF,)), dma((2,)),
-                dma((RP, U)), dma((RL,)), dma((RM,)),
+                dma((RP, U)), dma((RL, 2)), dma((RM,)),
                 pltpu.SemaphoreType.REGULAR, pltpu.SemaphoreType.REGULAR, pltpu.SemaphoreType.REGULAR,
             ],
             compiler_params=pltpu.CompilerParams(

time: 373 us -> 373 us (level)
  no operation moved by 1% of the time
where the time goes in v4:
time: 373 us; the launch traced here: 372 us
  Pallas kernels  372 us (100%)
    pallas_call x1, Pallas kernels, step(): pl.pallas_call(functools.partial(kernel, (nm, K, M, N)), out_shape=pltpu....  362 us
    pallas_call x1, Pallas kernels, step(): pl.pallas_call(put, out_shape=jax.ShapeDtypeStruct((nm, M, N), bf16), in_...  10.4 us

profile of v4, /device:TPU:3, one launch (start us, length us, event | category | flops | bytes accessed | tf_op | source)
XLA Modules:
  0.0 372.4 jit_solution(11647674475824933501)
XLA Ops:
  0.0 361.8 %shard_map.28.x = bf16[4,1280,3072]{2,1,0:T(8,128)(2,1)S(1)} custom-call(bf16[4,8192,1280]{2,1,0:T(8,128)(2,1)} %bitcast.a, bf16[4,8192,3072]{2,1,0:T(8,128)(2,1)} %bitcast.1.g), custom_call_target="tpu_custom_call" | custom-call | tf_op jit(solution)/shard_map/pallas_call | solution.py:399
  361.8 10.4 %shard_map.29 = bf16[4,1280,3072]{2,1,0:T(8,128)(2,1)} custom-call(bf16[4,1280,3072]{2,1,0:T(8,128)(2,1)S(1)} %shard_map.28.x), custom_call_target="tpu_custom_call" | custom-call | tf_op jit(solution)/shard_map/pallas_call | solution.py:424

commit v5 on v4

--- a/solution.py
+++ b/solution.py
@@ -13,8 +13,8 @@
 U = 2
 HALF, CH, CW = BM // 2, BM // 8, 2 * BN // U
 WC = BN // CW
-ND, NP, NS, NR, NF = 2, 4, 4, 2, 2
-RP, RL, RM = 3, 4, 7
+ND, NP, NS, NR, NF = 2, 4, 3, 2, 2
+RP, RL, RM = 2, 4, 7
 SUM, HELD = 4, 25
 PARTIAL = 5, 5
 FINISH = 9, 6
@@ -49,17 +49,10 @@
     inner = jnp.logical_not(leaf)
     rq, sq = sd, 1 - sd
     mate = (rep, z * 2 + 1 - c)
-    near = (rep, jnp.where(leaf, 1 + sd, 3 * sd) * 2 + c)
-    peer = (rep, (2 - sd) * 2 + c)
+    near = (rep, jnp.where(leaf, 1 + sd, 3 * sd) * 2 + 1 - c)
+    peer = (rep, (2 - sd) * 2 + 1 - c)
+    own = lax.rem(c + z, 2)
     f32, bf16 = jnp.float32, jnp.bfloat16
-
-    bar = pltpu.get_barrier_semaphore()
-    pl.semaphore_signal(bar, inc=1, device_id=mate, device_id_type=MESH)
-    pl.semaphore_signal(bar, inc=1, device_id=near, device_id_type=MESH)
-
-    @pl.when(inner)
-    def _():
-        pl.semaphore_signal(bar, inc=1, device_id=peer, device_id_type=MESH)
 
     def start(p):
         n, i, j = div(p, I * J), rem(div(p, J), I), rem(p, J)
@@ -92,6 +85,14 @@
             afirst(k, f).start()
             gfirst(k, f).start()
 
+    bar = pltpu.get_barrier_semaphore()
+    pl.semaphore_signal(bar, inc=1, device_id=mate, device_id_type=MESH)
+    pl.semaphore_signal(bar, inc=1, device_id=near, device_id_type=MESH)
+
+    @pl.when(inner)
+    def _():
+        pl.semaphore_signal(bar, inc=1, device_id=peer, device_id_type=MESH)
+
     def remote(src, dst, s, r, who):
         return pltpu.make_async_remote_copy(src, dst, s, r, device_id=who, device_id_type=MESH)
 
@@ -114,7 +115,7 @@
 
         def message(self, q, h):
             n, row, col = self.place
-            row, col = row + c * HALF + (2 * q + h // WC) * CH, col + h % WC * CW
+            row, col = row + own * HALF + (2 * q + h // WC) * CH, col + h % WC * CW
             return out.at[n, pl.ds(whole_of(row, 16), CH), pl.ds(whole_of(col, 128), CW)]
 
         def d_copy(self):
@@ -142,7 +143,7 @@
             return remote(at, at, f_sl.at[self.slot(NF)], lt_r.at[self.slot(RL), 1], near)
 
         def m_copy(self, q):
-            at = self.block(c, q)
+            at = self.block(own, q)
             return remote(at, at, m_s.at[self.slot(2)], m_r.at[self.slot(RM)], mate)
 
         def l_sent(self):
@@ -154,24 +155,24 @@
             remote(psend.at[s], precv.at[s], p_s.at[s], p_r.at[s, 0], peer).wait_send()
 
         def t_sent(self):
-            s, at = self.slot(NF), self.block(c, rq)
+            s, at = self.slot(NF), self.block(own, rq)
             remote(at, at, t_sp.at[s], pt_r.at[0, 0], peer).wait_send()
             remote(at, at, t_sl.at[s], lt_r.at[0, 0], near).wait_send()
 
         def f_sent(self):
-            at = self.block(c, sq)
+            at = self.block(own, sq)
             remote(at, at, f_sl.at[self.slot(NF)], lt_r.at[0, 0], near).wait_send()
 
         def m_sent(self):
-            at = self.half(c)
+            at = self.half(own)
             remote(at, at, m_s.at[self.slot(2)], m_r.at[0], mate).wait_send()
 
         def whole(self, k, q):
-            at = self.block(c, q)
+            at = self.block(own, q)
             remote(at, at, t_sl.at[0], lt_r.at[self.slot(RL), k], near).wait_recv()
 
         def given(self):
-            at = self.half(1 - c)
+            at = self.half(1 - own)
             remote(at, at, m_s.at[0], m_r.at[self.slot(RM)], mate).wait_recv()
 
     def multiply(p, k):
@@ -216,11 +217,11 @@
 
         for h in range(U):
             for q in range(2):
-                dout[s, h, q] = part(1 - c, h, q).astype(bf16)
+                dout[s, h, q] = part(1 - own, h, q).astype(bf16)
         it.d_copy().start()
         for h in range(U):
             for q in range(2):
-                pend[ps, h, q] = part(c, h, q)
+                pend[ps, h, q] = part(own, h, q)
 
     def chip_sum(it):
         it.d_copy().wait_recv()
@@ -338,8 +339,9 @@
         gcopy(1, k).start()
     pl.semaphore_wait(bar, jnp.where(leaf, 2, 3))
     swap(Piece(0, False))
-
-    lax.fori_loop(1, HEAD, functools.partial(step, "head"), 0)
+    step("head", 1, 0)
+
+    lax.fori_loop(2, HEAD, functools.partial(step, "head"), 0)
     lax.fori_loop(HEAD, total, functools.partial(step, "body"), 0)
 
     def tail(p, _):

time: 373 us -> 372 us (level)
  no operation moved by 1% of the time
where the time goes in v5:
time: 372 us
  Pallas kernels  372 us (100%)
    pallas_call x1, Pallas kernels, step(): pl.pallas_call(functools.partial(kernel, (nm, K, M, N)), out_shape=pltpu....  362 us
    pallas_call x1, Pallas kernels, step(): pl.pallas_call(put, out_shape=jax.ShapeDtypeStruct((nm, M, N), bf16), in_...  10.4 us

profile of v5, /device:TPU:3, one launch (start us, length us, event | category | flops | bytes accessed | tf_op | source)
XLA Modules:
  0.0 372.3 jit_solution(13507394671434093973)
XLA Ops:
  0.0 361.7 %shard_map.28.x = bf16[4,1280,3072]{2,1,0:T(8,128)(2,1)S(1)} custom-call(bf16[4,8192,1280]{2,1,0:T(8,128)(2,1)} %bitcast.a, bf16[4,8192,3072]{2,1,0:T(8,128)(2,1)} %bitcast.1.g), custom_call_target="tpu_custom_call" | custom-call | tf_op jit(solution)/shard_map/pallas_call | solution.py:401
  361.7 10.4 %shard_map.29 = bf16[4,1280,3072]{2,1,0:T(8,128)(2,1)} custom-call(bf16[4,1280,3072]{2,1,0:T(8,128)(2,1)S(1)} %shard_map.28.x), custom_call_target="tpu_custom_call" | custom-call | tf_op jit(solution)/shard_map/pallas_call | solution.py:426
